TPU v7x, 256 devices: a whole 4x4x8 slice. The times are simulated.
256 devices in a mesh: row: 16 (over y, x), col: 16 (over z, core).
Axes of the slice: x: 4, y: 4, z: 8, core: 2. Of those that a mesh axis runs over, the one named last changes fastest.
Arguments:
- tokens: bfloat16 [1024, 7168], P('col', 'row'), may hold values from -6 to 6
- routes: int32 [1024, 8], P('col'), may hold values from 0 to 31, all different within a row; in each aligned block of 64 rows (0 to 63, 64 to 127, ...) at most 40 rows name the same one
- gates: float32 [1024, 8], P('col'), may hold values from 0.05 to 0.5
- w_gate: bfloat16 [32, 7168, 2048], P('col', None, 'row'), may hold values from -0.0625 to 0.0625
- w_up: bfloat16 [32, 7168, 2048], P('col', None, 'row'), may hold values from -0.0625 to 0.0625
- w_down: bfloat16 [32, 2048, 7168], P('col', 'row'), may hold values from -0.125 to 0.125
Outputs:
- mixed: bfloat16 [1024, 7168], P('col', 'row')
Inputs may be any that keep to these rules, and one draw needn't show every extreme that they name: `routes`: the 8 experts of a token are distinct. Among the 64 tokens of one index of col (aligned blocks of 64 tokens), no expert is chosen more than 40 times, and some expert is chosen exactly 40 times.
All inputs are finite; a program needn't handle non-finite values.
Results may differ from a plain program's by a relative error of at most 0.015.
Values may be sent and summed in bfloat16 or wider, within the bound.
No kernel may reach another device: no remote copies, remote signals or barrier semaphores. Data moves between devices by JAX's collectives and lax.ppermute only.
A program may use at most 128 MiB of HBM per device.

v0:
```python
import jax
import jax.numpy as jnp
from jax import lax
from jax.sharding import PartitionSpec as P

CAP = 40


def group_positions(grouped, expert_count):
    onehot = (
        grouped[:, :, None] == jnp.arange(expert_count, dtype=jnp.int32)[None, None, :]
    ).astype(jnp.int32)
    before = jnp.cumsum(onehot, axis=1) - onehot
    return jnp.sum(before * onehot, axis=2)


def shards(tokens, routes, gates, w_gate, w_up, w_down):
    held_experts = w_gate.shape[0]
    unit_count = w_gate.shape[2]
    group_count = lax.axis_size("col")
    expert_count = held_experts * group_count
    tok_rows, top_count = routes.shape
    slot_count = CAP * group_count
    flat_routes = routes.reshape(1, tok_rows * top_count)
    position = group_positions(flat_routes, expert_count)[0]
    target = flat_routes[0] * CAP + position
    owner_rows = jnp.arange(tok_rows * top_count, dtype=jnp.int32) // top_count
    outgoing = jnp.zeros((expert_count * CAP, tokens.shape[1]), jnp.bfloat16)
    outgoing = (
        outgoing.at[target].set(tokens[owner_rows]).reshape(expert_count, CAP, tokens.shape[1])
    )
    arrived = lax.all_to_all(outgoing, "col", split_axis=0, concat_axis=1, tiled=True)
    piece = lax.all_gather(arrived, "row", axis=2, tiled=True)
    gate_act = jnp.einsum("erd,edf->erf", piece, w_gate, preferred_element_type=jnp.float32)
    up_act = jnp.einsum("erd,edf->erf", piece, w_up, preferred_element_type=jnp.float32)
    hidden = (jax.nn.silu(gate_act) * up_act).astype(jnp.bfloat16)
    columns = lax.all_to_all(w_down, "row", split_axis=2, concat_axis=1, tiled=True)
    wide_hidden = lax.all_gather(hidden, "row", axis=2, tiled=True)
    blocks = lax.axis_size("row")
    partial_value = jnp.einsum(
        "ercf,ecfd->ecrd",
        wide_hidden.reshape(held_experts, slot_count, blocks, unit_count),
        columns.reshape(held_experts, blocks, unit_count, columns.shape[2]),
        preferred_element_type=jnp.float32,
    )
    rounded = lax.optimization_barrier(partial_value.astype(jnp.bfloat16))
    result = jnp.sum(rounded.astype(jnp.float32), axis=1).astype(jnp.bfloat16)
    returned = lax.all_to_all(result, "col", split_axis=1, concat_axis=0, tiled=True)
    picked = returned.reshape(expert_count * CAP, returned.shape[2])[target]
    picked = picked.reshape(tok_rows, top_count, returned.shape[2])
    mixed = jnp.sum(gates[:, :, None] * picked.astype(jnp.float32), axis=1)
    return mixed.astype(jnp.bfloat16)


def solution(mesh):
    return jax.shard_map(
        shards,
        mesh=mesh,
        in_specs=(
            P("col", "row"),
            P("col", None),
            P("col", None),
            P("col", None, "row"),
            P("col", None, "row"),
            P("col", "row", None),
        ),
        out_specs=P("col", "row"),
        check_vma=False,
    )
```

profile of v0, /device:TPU:1, one launch (start us, length us, event | category | flops | bytes accessed | tf_op | source)
XLA Modules:
  0.0 376.0 jit_solution(8991820587349833042)
XLA Ops:
  6.5 0.0 copy-start
  6.5 0.0 all-gather.3.cloned.1.call-start
  6.5 0.8 copy.23
  7.3 0.1 eq.27
  7.4 0.1 compare_convert_fusion
  7.5 1.2 reduce-window.6
  8.7 0.2 slice_reduce_fusion
  8.9 0.1 copy.25
  9.0 0.7 broadcast_multiply_fusion
  9.7 0.1 copy.26
  9.8 0.1 copy.22
  9.9 0.1 mul.37
  10.0 0.1 broadcast.138
  10.1 0.1 fusion.7
  10.2 0.0 copy-done
  10.2 5.2 %scatter_custom_fusion = bf16[1280,448]{1,0:T(8,128)(2,1)S(1)} fusion(s32[512]{0:T(512)S(1)} %bitcast.54, bf16[]{:T(256)} %constant.27.clone.1, bf16[64,448]{1,0:T(8,128)(2,1)S(1)} %copy-done, s32[1024]{0:T(1024)S(1)} %pad_clamp_fusion.1), kind=kCustom, calls=%fused_computation.10 | custom fusion | bytes 1146882 | tf_op jit(solution)/shard_map/scatter | solution.py:30
  15.4 43.8 %all_to_all.48 = bf16[32,40,448]{2,1,0:T(8,128)(2,1)S(1)} all-to-all(bf16[32,40,448]{2,1,0:T(8,128)(2,1)S(1)} %bitcast.46), channel_id=1, replica_groups=mesh['row'=16,'col'=16] {'col'}, dimensions={0} | all-to-all | bytes 2293760 | tf_op jit(solution)/shard_map/all_to_all | solution.py:32
  59.2 0.1 copy.27
  59.3 1.4 copy.28
  60.8 0.0 all-gather.3.cloned.1.call-update
  60.8 0.2 all-gather.5.cloned.1.call-start
  61.0 120.8 %all-gather.3.cloned.1.call-done = bf16[2,640,7168]{1,2,0:T(8,128)(2,1)} async-done(((bf16[2,640,448]{1,2,0:T(8,128)(2,1)}), bf16[2,640,7168]{1,2,0:T(8,128)(2,1)}) %all-gather.3.cloned.1.call-update) | async-done | bytes 18350096 | tf_op jit(solution)/shard_map/all_gather | solution.py:33
  181.8 0.0 copy-start.2
  181.8 11.6 %fusion.8 = f32[2,640,128]{2,1,0:T(8,128)S(1)} fusion(bf16[2,640,7168]{1,2,0:T(8,128)(2,1)} %all-gather.3.cloned.1.call-done, bf16[2,7168,128]{2,1,0:T(8,128)(2,1)} %param.9), kind=kOutput, calls=%fused_computation.28 | convolution fusion | flops 2348810240 | bytes 22675456 | tf_op jit(solution)/shard_map/erd,edf->erf/dot_general | solution.py:34
  193.4 0.0 copy-done.2
  193.5 11.9 %fusion.2 = bf16[2,640,128]{2,1,0:T(8,128)(2,1)} fusion(bf16[2,640,7168]{1,2,0:T(8,128)(2,1)} %all-gather.3.cloned.1.call-done, bf16[2,7168,128]{2,1,0:T(8,128)(2,1)S(1)} %copy-done.2, f32[2,640,128]{2,1,0:T(8,128)S(1)} %fusion.8), kind=kOutput, calls=%fused_computation.7 | convolution fusion | flops 2349793280 | bytes 23003136 | tf_op jit(solution)/shard_map/erd,edf->erf/dot_general | solution.py:35
  205.3 0.0 all-gather.5.cloned.1.call-update
  205.3 9.9 %copy.29 = bf16[2,128,7168]{1,0,2:T(2,128)(2,1)} copy(bf16[2,128,7168]{2,1,0:T(8,128)(2,1)} %param.11) | data formatting | bytes 7340032 | tf_op args[5]
  215.2 52.8 %all_to_all.49 = bf16[2,128,7168]{1,0,2:T(2,128)(2,1)S(1)} all-to-all(bf16[2,128,7168]{1,0,2:T(2,128)(2,1)} %copy.29), channel_id=1, replica_groups=mesh['row'=16,'col'=16] {'row'}, dimensions={2} | all-to-all | bytes 7340032 | tf_op jit(solution)/shard_map/all_to_all | solution.py:37
  268.0 2.4 copy.30
  270.4 28.9 %all-gather.5.cloned.1.call-done = bf16[2,640,2048]{2,1,0:T(8,128)(2,1)} async-done(((bf16[2,640,128]{2,1,0:T(8,128)(2,1)}), bf16[2,640,2048]{2,1,0:T(8,128)(2,1)}) %all-gather.5.cloned.1.call-update) | async-done | bytes 5242896 | tf_op jit(solution)/shard_map/all_gather | solution.py:38
  299.2 12.0 %convolution_convert_fusion = bf16[2,16,640,448]{2,3,1,0:T(8,128)(2,1)} fusion(bf16[2,16,128,448]{2,3,1,0:T(8,128)(2,1)} %bitcast.44, bf16[2,640,2048]{2,1,0:T(8,128)(2,1)} %all-gather.5.cloned.1.call-done), kind=kOutput, calls=%fused_computation.3 | convolution fusion | flops 2357985280 | bytes 27262976 | tf_op jit(solution)/shard_map/ercf,ecfd->ecrd/dot_general | solution.py:40
  311.2 9.4 %reduce_sum.34 = bf16[2,640,448]{1,2,0:T(8,128)(2,1)S(1)} reduce(bf16[2,16,640,448]{2,3,1,0:T(8,128)(2,1)} %convolution_convert_fusion, bf16[]{:T(256)} %constant.27.clone.1), dimensions={1}, to_apply=%region_4.5 | reduce | flops 8601600 | bytes 19496962 | tf_op jit(solution)/shard_map/reduce_sum | solution.py:47
  320.7 0.0 copy-start.3
  320.7 2.8 copy.32
  323.5 9.1 %all-to-all-start.2 = ((bf16[2,640,448]{2,0,1:T(2,128)(2,1)}), bf16[2,640,448]{2,0,1:T(2,128)(2,1)S(1)}, u32[]{:S(2)}, u32[]{:S(2)}) async-start(bf16[2,640,448]{2,0,1:T(2,128)(2,1)} %copy.32), calls=%async_computation.2 | async-start | bytes 2621440 | tf_op jit(solution)/shard_map/all_to_all | solution.py:48
  332.5 0.0 copy-done.3
  332.5 0.1 copy.21
  332.6 33.2 %all-to-all-done.2 = bf16[2,640,448]{2,0,1:T(2,128)(2,1)S(1)} async-done(((bf16[2,640,448]{2,0,1:T(2,128)(2,1)}), bf16[2,640,448]{2,0,1:T(2,128)(2,1)S(1)}, u32[]{:S(2)}, u32[]{:S(2)}) %all-to-all-start.2) | async-done | bytes 1146912 | tf_op jit(solution)/shard_map/all_to_all | solution.py:48
  365.8 0.2 copy.33
  366.0 0.0 copy-start.1
  366.0 0.1 copy.34
  366.1 2.0 gather_fusion
  368.1 1.0 fusion.3
  369.1 0.0 copy-done.1
  (7 shorter events, 0.1 us)
Async XLA Ops:
  6.5 3.7 copy-start
  6.5 175.3 %all-gather.3.cloned.1.call-start = ((), (), s32[]{:S(2)}) async-start(), calls=%async_computation.3 | async-start | bytes 19496960 | tf_op jit(solution)/shard_map/all_gather | solution.py:33
  60.8 238.5 %all-gather.5.cloned.1.call-start = ((), (), s32[]{:S(2)}) async-start(), calls=%async_computation.4 | async-start | bytes 5570560 | tf_op jit(solution)/shard_map/all_gather | solution.py:38
  181.8 11.6 %copy-start.2 = (bf16[2,7168,128]{2,1,0:T(8,128)(2,1)S(1)}, bf16[2,7168,128]{2,1,0:T(8,128)(2,1)}, u32[]{:S(2)}) copy-start(bf16[2,7168,128]{2,1,0:T(8,128)(2,1)} %param.10) | copy-start | bytes 11010052
  320.7 11.9 %copy-start.3 = (f32[64,8]{0,1:T(8,128)S(1)}, f32[64,8]{0,1:T(8,128)}, u32[]{:S(2)}) copy-start(f32[64,8]{0,1:T(8,128)} %param.8) | copy-start | bytes 6148
  323.5 42.3 %all-to-all-start.2 = ((bf16[2,640,448]{2,0,1:T(2,128)(2,1)}), bf16[2,640,448]{2,0,1:T(2,128)(2,1)S(1)}, u32[]{:S(2)}, u32[]{:S(2)}) async-start(bf16[2,640,448]{2,0,1:T(2,128)(2,1)} %copy.32), calls=%async_computation.2 | async-start | bytes 2621440 | tf_op jit(solution)/shard_map/all_to_all | solution.py:48
  366.0 3.2 copy-start.1
Sparse Core Ops, SparseCore 0:
  60.9 120.8 all-gather.2
  205.5 93.7 all-gather.4
where the time goes:
time: 377 us; the launch traced here: 376 us
  waiting for transfers between devices  183 us (49%)
  blocking collectives  96.6 us (26%)
  matrix products  35.5 us (9%)
  local copies, waits for them, and re-layouts  25.7 us (7%)
  between operations  13.5 us (4%)
  other arithmetic  12.6 us (3%)
  starting transfers between devices  9.29 us (2%)
    all_gather x1, waiting for transfers between devices, shards(): piece = lax.all_gather(arrived, 'row', axis=2, tiled=True)  121 us
    all_to_all x1, blocking collectives, shards(): lax.all_to_all(w_down, 'row', split_axis=2, concat_axis=1, tiled=True)  52.8 us
    all_to_all x1, blocking collectives, shards(): lax.all_to_all(outgoing, 'col', split_axis=0, concat_axis=1, tiled=True)  43.8 us
    all_to_all x1, waiting for transfers between devices, shards(): lax.all_to_all(result, 'col', split_axis=1, concat_axis=0, tiled=True)  33.2 us
    all_gather x1, waiting for transfers between devices, shards(): wide_hidden = lax.all_gather(hidden, 'row', axis=2, tiled=True)  28.9 us
    dot_general x1, matrix products, shards(): jnp.einsum('ercf,ecfd->ecrd', wide_hidden.reshape(held_experts, slot_coun...  12 us
    dot_general x1, matrix products, shards(): jnp.einsum('erd,edf->erf', piece, w_up, preferred_element_type=jnp.float32)  11.9 us
    dot_general x1, matrix products, shards(): jnp.einsum('erd,edf->erf', piece, w_gate, preferred_element_type=jnp.floa...  11.6 us
  transfers between devices with their start and end apart: 3, of which 3 were waited for; matrix products, arithmetic and copies ran while one was open for 3% of the time, Pallas kernels for 0%

commit v1 on v0

--- a/solution.py
+++ b/solution.py
@@ -30,7 +30,9 @@
         outgoing.at[target].set(tokens[owner_rows]).reshape(expert_count, CAP, tokens.shape[1])
     )
     arrived = lax.all_to_all(outgoing, "col", split_axis=0, concat_axis=1, tiled=True)
-    piece = lax.all_gather(arrived, "row", axis=2, tiled=True)
+    piece = jnp.concatenate(
+        lax.all_to_all(jnp.stack([arrived] * lax.axis_size("row")), "row", 0, 0), axis=2
+    )
     gate_act = jnp.einsum("erd,edf->erf", piece, w_gate, preferred_element_type=jnp.float32)
     up_act = jnp.einsum("erd,edf->erf", piece, w_up, preferred_element_type=jnp.float32)
     hidden = (jax.nn.silu(gate_act) * up_act).astype(jnp.bfloat16)

time: 377 us -> 474 us (1.26)
  blocking collectives: 96.6 us -> 306 us
  waiting for transfers between devices: 183 us -> 63.3 us
  local copies, waits for them, and re-layouts: 25.7 us -> 34.2 us
    all_to_all x0 -> x1, blocking collectives: none -> 210 us  [shards(): lax.all_to_all(jnp.stack([arrived] * lax.axis_size('row')), 'row', 0, 0)]
    all_gather x1 -> x0, waiting for transfers between devices: 121 us -> none  [shards(): piece = lax.all_gather(arrived, 'row', axis=2, tiled=True)]
    all_to_all x0 -> x1, local copies, waits for them, and re-layouts: none -> 6.95 us  [shards(): lax.all_to_all(jnp.stack([arrived] * lax.axis_size('row')), 'row', 0, 0)]
    unnamed x11 -> x13, local copies, waits for them, and re-layouts: 10.8 us -> 10.8 us
  transfers between devices with their start and end apart: 3 -> 2, of which waited for: 3 -> 2; matrix products, arithmetic and copies ran while one was open for 3% -> 3% of each run, Pallas kernels for 0% -> 0%
where the time goes in v1:
time: 474 us; the launch traced here: 473 us
  blocking collectives  306 us (65%)
  waiting for transfers between devices  63.3 us (13%)
  matrix products  35 us (7%)
  local copies, waits for them, and re-layouts  34.2 us (7%)
  between operations  13.5 us (3%)
  other arithmetic  12.6 us (3%)
  starting transfers between devices  9.06 us (2%)
    all_to_all x1, blocking collectives, shards(): lax.all_to_all(jnp.stack([arrived] * lax.axis_size('row')), 'row', 0, 0)  210 us
    all_to_all x1, blocking collectives, shards(): lax.all_to_all(w_down, 'row', split_axis=2, concat_axis=1, tiled=True)  51.3 us
    all_to_all x1, blocking collectives, shards(): lax.all_to_all(outgoing, 'col', split_axis=0, concat_axis=1, tiled=True)  43.8 us
    all_to_all x1, waiting for transfers between devices, shards(): lax.all_to_all(result, 'col', split_axis=1, concat_axis=0, tiled=True)  33.2 us
    all_gather x1, waiting for transfers between devices, shards(): wide_hidden = lax.all_gather(hidden, 'row', axis=2, tiled=True)  30.1 us
    dot_general x1, matrix products, shards(): jnp.einsum('ercf,ecfd->ecrd', wide_hidden.reshape(held_experts, slot_coun...  12 us
    dot_general x1, matrix products, shards(): jnp.einsum('erd,edf->erf', piece, w_up, preferred_element_type=jnp.float32)  11.9 us
    dot_general x1, matrix products, shards(): jnp.einsum('erd,edf->erf', piece, w_gate, preferred_element_type=jnp.floa...  11.2 us
  transfers between devices with their start and end apart: 2, of which 2 were waited for; matrix products, arithmetic and copies ran while one was open for 3% of the time, Pallas kernels for 0%

profile of v1, /device:TPU:1, one launch (start us, length us, event | category | flops | bytes accessed | tf_op | source)
XLA Modules:
  0.0 473.2 jit_solution(10824859618947674513)
XLA Ops:
  6.5 0.0 copy-start
  6.5 0.0 all-gather.2.cloned.1.call-start
  6.5 0.8 copy.36
  7.3 0.1 eq.27
  7.4 0.1 compare_convert_fusion
  7.5 1.2 reduce-window.6
  8.7 0.2 slice_reduce_fusion
  8.9 0.1 copy.38
  9.0 0.7 broadcast_multiply_fusion
  9.7 0.1 copy.39
  9.8 0.1 copy.35
  9.9 0.1 mul.37
  10.0 0.1 broadcast.139
  10.1 0.1 fusion.7
  10.2 0.0 copy-done
  10.2 5.2 %scatter_custom_fusion = bf16[1280,448]{1,0:T(8,128)(2,1)S(1)} fusion(s32[512]{0:T(512)S(1)} %bitcast.59, bf16[]{:T(256)} %constant.27.clone.1, bf16[64,448]{1,0:T(8,128)(2,1)S(1)} %copy-done, s32[1024]{0:T(1024)S(1)} %pad_clamp_fusion.1), kind=kCustom, calls=%fused_computation.10 | custom fusion | bytes 1146882 | tf_op jit(solution)/shard_map/scatter | solution.py:30
  15.4 43.8 %all_to_all.50 = bf16[32,40,448]{2,1,0:T(8,128)(2,1)S(1)} all-to-all(bf16[32,40,448]{2,1,0:T(8,128)(2,1)S(1)} %bitcast.51), channel_id=1, replica_groups=mesh['row'=16,'col'=16] {'col'}, dimensions={0} | all-to-all | bytes 2293760 | tf_op jit(solution)/shard_map/all_to_all | solution.py:32
  59.2 0.1 copy.40
  59.3 0.7 copy.41
  60.1 2.3 stack.5
  62.3 210.5 %all_to_all.51 = bf16[16,2,640,448]{2,3,1,0:T(8,128)(2,1)S(1)} all-to-all(bf16[16,2,640,448]{2,3,1,0:T(8,128)(2,1)S(1)} %stack.5), channel_id=1, replica_groups=mesh['row'=16,'col'=16] {'row'}, dimensions={0} | all-to-all | bytes 36700160 | tf_op jit(solution)/shard_map/all_to_all | solution.py:34
  272.8 0.0 copy-start.2
  272.8 6.9 %copy.42 = bf16[16,2,640,448]{2,3,0,1:T(8,128)(2,1)} copy(bf16[16,2,640,448]{2,3,1,0:T(8,128)(2,1)S(1)} %all_to_all.51) | data formatting | bytes 36700160 | tf_op jit(solution)/shard_map/all_to_all | solution.py:34
  279.8 0.0 copy-done.2
  279.8 0.0 copy-start.3
  279.8 11.2 %fusion.8 = f32[2,640,128]{2,1,0:T(8,128)S(1)} fusion(bf16[2,640,7168]{1,2,0:T(8,128)(2,1)} %bitcast.47, bf16[2,7168,128]{2,1,0:T(8,128)(2,1)S(1)} %copy-done.2), kind=kOutput, calls=%fused_computation.28 | convolution fusion | flops 2348810240 | bytes 22675456 | tf_op jit(solution)/shard_map/erd,edf->erf/dot_general | solution.py:36
  291.0 0.0 copy-done.3
  291.0 11.9 %fusion.2 = bf16[2,640,128]{2,1,0:T(8,128)(2,1)} fusion(bf16[2,640,7168]{1,2,0:T(8,128)(2,1)} %bitcast.48, bf16[2,7168,128]{2,1,0:T(8,128)(2,1)S(1)} %copy-done.3, f32[2,640,128]{2,1,0:T(8,128)S(1)} %fusion.8), kind=kOutput, calls=%fused_computation.7 | convolution fusion | flops 2349793280 | bytes 23003136 | tf_op jit(solution)/shard_map/erd,edf->erf/dot_general | solution.py:37
  302.8 0.0 all-gather.2.cloned.1.call-update
  302.9 9.9 %copy.45 = bf16[2,128,7168]{1,0,2:T(2,128)(2,1)} copy(bf16[2,128,7168]{2,1,0:T(8,128)(2,1)} %param.11) | data formatting | bytes 7340032 | tf_op args[5]
  312.8 51.3 %all_to_all.52 = bf16[2,128,7168]{1,0,2:T(2,128)(2,1)S(1)} all-to-all(bf16[2,128,7168]{1,0,2:T(2,128)(2,1)} %copy.45), channel_id=1, replica_groups=mesh['row'=16,'col'=16] {'row'}, dimensions={2} | all-to-all | bytes 7340032 | tf_op jit(solution)/shard_map/all_to_all | solution.py:39
  364.1 2.4 copy.46
  366.4 30.1 %all-gather.2.cloned.1.call-done = bf16[2,640,2048]{2,1,0:T(8,128)(2,1)} async-done(((bf16[2,640,128]{2,1,0:T(8,128)(2,1)}), bf16[2,640,2048]{2,1,0:T(8,128)(2,1)}) %all-gather.2.cloned.1.call-update) | async-done | bytes 5242896 | tf_op jit(solution)/shard_map/all_gather | solution.py:40
  396.5 12.0 %convolution_convert_fusion = bf16[2,16,640,448]{2,3,1,0:T(8,128)(2,1)} fusion(bf16[2,16,128,448]{2,3,1,0:T(8,128)(2,1)} %bitcast.49, bf16[2,640,2048]{2,1,0:T(8,128)(2,1)} %all-gather.2.cloned.1.call-done), kind=kOutput, calls=%fused_computation.3 | convolution fusion | flops 2357985280 | bytes 27262976 | tf_op jit(solution)/shard_map/ercf,ecfd->ecrd/dot_general | solution.py:42
  408.5 9.4 %reduce_sum.34 = bf16[2,640,448]{1,2,0:T(8,128)(2,1)S(1)} reduce(bf16[2,16,640,448]{2,3,1,0:T(8,128)(2,1)} %convolution_convert_fusion, bf16[]{:T(256)} %constant.27.clone.1), dimensions={1}, to_apply=%region_4.5 | reduce | flops 8601600 | bytes 19496962 | tf_op jit(solution)/shard_map/reduce_sum | solution.py:49
  417.9 0.0 copy-start.4
  417.9 2.8 copy.48
  420.7 9.1 %all-to-all-start.3 = ((bf16[2,640,448]{2,0,1:T(2,128)(2,1)}), bf16[2,640,448]{2,0,1:T(2,128)(2,1)S(1)}, u32[]{:S(2)}, u32[]{:S(2)}) async-start(bf16[2,640,448]{2,0,1:T(2,128)(2,1)} %copy.48), calls=%async_computation.3 | async-start | bytes 2621440 | tf_op jit(solution)/shard_map/all_to_all | solution.py:50
  429.8 0.0 copy-done.4
  429.8 0.1 copy.34
  429.9 33.2 %all-to-all-done.3 = bf16[2,640,448]{2,0,1:T(2,128)(2,1)S(1)} async-done(((bf16[2,640,448]{2,0,1:T(2,128)(2,1)}), bf16[2,640,448]{2,0,1:T(2,128)(2,1)S(1)}, u32[]{:S(2)}, u32[]{:S(2)}) %all-to-all-start.3) | async-done | bytes 1146912 | tf_op jit(solution)/shard_map/all_to_all | solution.py:50
  463.0 0.2 copy.49
  463.2 0.0 copy-start.1
  463.3 0.1 copy.50
  463.4 2.0 gather_fusion
  465.4 1.0 fusion.3
  466.4 0.0 copy-done.1
  (7 shorter events, 0.1 us)
Async XLA Ops:
  6.5 3.7 copy-start
  6.5 390.0 %all-gather.2.cloned.1.call-start = ((), (), s32[]{:S(2)}) async-start(), calls=%async_computation.4 | async-start | bytes 5570560 | tf_op jit(solution)/shard_map/all_gather | solution.py:40
  272.8 7.0 %copy-start.2 = (bf16[2,7168,128]{2,1,0:T(8,128)(2,1)S(1)}, bf16[2,7168,128]{2,1,0:T(8,128)(2,1)}, u32[]{:S(2)}) copy-start(bf16[2,7168,128]{2,1,0:T(8,128)(2,1)} %param.9) | copy-start | bytes 11010052
  279.8 11.2 %copy-start.3 = (bf16[2,7168,128]{2,1,0:T(8,128)(2,1)S(1)}, bf16[2,7168,128]{2,1,0:T(8,128)(2,1)}, u32[]{:S(2)}) copy-start(bf16[2,7168,128]{2,1,0:T(8,128)(2,1)} %param.10) | copy-start | bytes 11010052
  417.9 11.8 %copy-start.4 = (f32[64,8]{0,1:T(8,128)S(1)}, f32[64,8]{0,1:T(8,128)}, u32[]{:S(2)}) copy-start(f32[64,8]{0,1:T(8,128)} %param.8) | copy-start | bytes 6148
  420.7 42.3 %all-to-all-start.3 = ((bf16[2,640,448]{2,0,1:T(2,128)(2,1)}), bf16[2,640,448]{2,0,1:T(2,128)(2,1)S(1)}, u32[]{:S(2)}, u32[]{:S(2)}) async-start(bf16[2,640,448]{2,0,1:T(2,128)(2,1)} %copy.48), calls=%async_computation.3 | async-start | bytes 2621440 | tf_op jit(solution)/shard_map/all_to_all | solution.py:50
  463.2 3.2 copy-start.1
Sparse Core Ops, SparseCore 0:
  303.0 93.4 all-gather.1
